TPU v7x, 32 devices: a whole 2x2x4 slice. The times are simulated.
32 devices in a mesh: gx: 8 (over y, x, core), gy: 4 (over z).
Axes of the slice: x: 2, y: 2, z: 4, core: 2. Of those that a mesh axis runs over, the one named last changes fastest.
Arguments:
- rhs: float32 [8, 125, 512], P('gx', None, 'gy'), may hold values from -6 to 6
- inverse: bfloat16 [8, 125, 125, 512], P('gx', None, None, 'gy')
- weights: float32 [8, 4, 512], P('gx', None, 'gy'), may hold values from 0.12 to 0.3
- neighbours: int32 [8, 4, 512], P('gx', None, 'gy'), may hold values from 0 to 383, as said below
- send_lists: int32 [8, 4, 256], P('gx', None, 'gy'), may hold values from 0 to 127
- coloring: int32 [8, 4], P('gx', 'gy'), may hold values from 0 to 3, as said below
Outputs:
- solution: float32 [8, 125, 512], P('gx', None, 'gy')
- norms: float32 [2], replicated
Inputs may be any that keep to these rules, and one draw needn't show every extreme that they name: `coloring`: the color of subdomain (i, j) depends only on i mod 2 and j mod 2, and the four parity classes have four different colors; which class has which color varies. `neighbours`: slots below 128 are the subdomain's own faces, the rest the received intersection faces in the order of the steps; every received slot is used by some face.
All inputs are finite; a program needn't handle non-finite values.
Results may differ from a plain program's by a relative error of at most 0.0055.
Values sent between devices are 32-bit elements; how exact they have to be, the bound alone decides.
No kernel may reach another device: no remote copies, remote signals or barrier semaphores. Data moves between devices by JAX's collectives and lax.ppermute only.
A program may use at most 64 MiB of HBM per device.

v0:
```python
import jax
import jax.numpy as jnp
from jax import lax
from jax.sharding import PartitionSpec as P

SWEEPS = 2


def from_behind(value, axis, steps):
    count = lax.axis_size(axis)
    leading, last = (max(0, -steps), min(count, count - steps))
    return lax.ppermute(value, axis, [(source, source + steps) for source in range(leading, last)])


def gather_margin(solution, sending):
    packs = [jnp.take(solution, sending[side], axis=1) for side in range(4)]
    below = from_behind(packs[0], "gx", 1)
    above = from_behind(packs[1], "gx", -1)
    left = from_behind(packs[2], "gy", 1)
    right_side = from_behind(packs[3], "gy", -1)
    return jnp.concatenate([solution, below, above, left, right_side], axis=1)


def body(rhs, inverse, weights, neighbours, send_lists, coloring):
    right = rhs[0]
    blocks = inverse[0]
    coupling = weights[0]
    slots = neighbours[0]
    sending = send_lists[0]
    own_color = coloring[0, 0]
    solution = jnp.zeros(right.shape, jnp.float32)
    locals_list = []

    def update(operands):
        extended, current = operands
        couple = jnp.zeros_like(current)
        for k in range(coupling.shape[0]):
            couple = couple + coupling[k][None, :] * jnp.take(extended, slots[k], axis=1)
        source = (right + couple).astype(jnp.bfloat16)
        candidate = jnp.einsum("ijf,jf->if", blocks, source, preferred_element_type=jnp.float32)
        delta = candidate - current
        return (candidate, jnp.sum(delta * delta))

    def unchanged(operands):
        return (operands[1], jnp.zeros((), jnp.float32))

    for sweep in range(SWEEPS):
        squares = jnp.zeros((), jnp.float32)
        for color in range(4):
            extended = gather_margin(solution, sending)
            solution, increment = lax.cond(
                own_color == color, update, unchanged, (extended, solution)
            )
            squares = squares + increment
        locals_list.append(squares)
    totals = lax.psum(jnp.stack(locals_list), ("gx", "gy"))
    norms = jnp.sqrt(totals)
    return (solution[None], norms)


def solution(mesh):
    in_specs = (
        P("gx", None, "gy"),
        P("gx", None, None, "gy"),
        P("gx", None, "gy"),
        P("gx", None, "gy"),
        P("gx", None, "gy"),
        P("gx", "gy"),
    )
    out_specs = (P("gx", None, "gy"), P())
    return jax.shard_map(body, mesh=mesh, in_specs=in_specs, out_specs=out_specs, check_vma=False)
```

profile of v0, /device:TPU:0, one launch (start us, length us, event | category | flops | bytes accessed | tf_op | source)
XLA Modules:
  0.0 275.8 jit_solution(7783205640333041183)
XLA Ops:
  2.2 2.4 collective-permute-start
  7.2 4.3 %collective-permute-start.2 = (f32[125,64]{0,1:T(8,128)S(1)}, f32[125,64]{0,1:T(8,128)S(1)}, u32[]{:S(2)}, u32[]{:S(2)}) collective-permute-start(f32[125,64]{0,1:T(8,128)S(1)} %select_bitcast_fusion.29), channel_id=1, source_target_pairs={{0,1},{1,2},{2,3},{4,5},{5,6},{6,7},{8,9},{9,10},{10,11},{12,13},{... | collective-permute-start | bytes 96008 | tf_op jit(solution)/shard_map/ppermute | solution.py:12
  15.2 2.8 %collective-permute-done.3 = f32[125,64]{0,1:T(8,128)S(1)} collective-permute-done((f32[125,64]{0,1:T(8,128)S(1)}, f32[125,64]{0,1:T(8,128)S(1)}, u32[]{:S(2)}, u32[]{:S(2)}) %collective-permute-start.3) | collective-permute-done | bytes 32032 | tf_op jit(solution)/shard_map/ppermute | solution.py:12
  18.0 19.4 %conditional.8 = (f32[125,128]{0,1:T(8,128)}, f32[]{:T(128)}, f32[125,128]{1,0:T(8,128)}) conditional(s32[]{:T(128)} %bitcast.108, () %tuple.78, (f32[4,128]{1,0:T(4,128)}, s32[4,128]{1,0:T(4,128)}, f32[125,384]{0,1:T(8,128)S(1)}, f32[125,128]{0,1:T(8,128)S(1)}, bf16[125,125,128]{2,1,0:T(8,128)(2,1)}) %tuple.265), branch_computations={%region_0.0_spmd.clone, %region_1.5_spmd.clone} | conditional | flops 4247167 | bytes 13183772 | solution.py:51
  22.5 7.2 %copy.42 = bf16[125,125,128]{0,1,2:T(8,128)(2,1)} copy(bf16[125,125,128]{2,1,0:T(8,128)(2,1)} %get-tuple-element.193) | data formatting | bytes 8000000 | tf_op jit(solution)/shard_map
  29.7 4.0 %fusion.5 = f32[128,1,125]{2,1,0:T(1,128)} fusion(bf16[125,125,128]{0,1,2:T(8,128)(2,1)} %copy.42, bf16[125,128,1]{0,1,2:T(8,128)(2,1)S(1)} %fusion.7), kind=kOutput, calls=%fused_computation.73 | convolution fusion | flops 4000000 | bytes 4096000 | tf_op jit(solution)/shard_map/cond/branch_1_fun/ijf,jf->if/dot_general | solution.py:40
  33.7 1.6 copy.94
  35.3 1.5 multiply_reduce_fusion
  49.6 3.3 %collective-permute-done.5 = f32[125,64]{0,1:T(8,128)S(1)} collective-permute-done((f32[125,64]{0,1:T(8,128)S(1)}, f32[125,64]{0,1:T(8,128)S(1)}, u32[]{:S(2)}, u32[]{:S(2)}) %collective-permute-start.5) | collective-permute-done | bytes 32032 | tf_op jit(solution)/shard_map/ppermute | solution.py:12
  52.9 2.9 %collective-permute-done.7 = f32[125,64]{0,1:T(8,128)S(1)} collective-permute-done((f32[125,64]{0,1:T(8,128)S(1)}, f32[125,64]{0,1:T(8,128)S(1)}, u32[]{:S(2)}, u32[]{:S(2)}) %collective-permute-start.7) | collective-permute-done | bytes 32032 | tf_op jit(solution)/shard_map/ppermute | solution.py:12
  59.2 17.7 %collective-permute-start.8 = (f32[125,64]{0,1:T(8,128)S(1)}, f32[125,64]{0,1:T(8,128)S(1)}, u32[]{:S(2)}, u32[]{:S(2)}) collective-permute-start(f32[125,64]{0,1:T(8,128)S(1)} %select_bitcast_fusion.23), channel_id=1, source_target_pairs={{0,4},{4,8},{8,12},{12,16},{16,20},{20,24},{24,28},{1,5},{5,9},{9,... | collective-permute-start | bytes 96008 | tf_op jit(solution)/shard_map/ppermute | solution.py:12
  81.3 5.1 %collective-permute-done.11 = f32[125,64]{0,1:T(8,128)S(1)} collective-permute-done((f32[125,64]{0,1:T(8,128)S(1)}, f32[125,64]{0,1:T(8,128)S(1)}, u32[]{:S(2)}, u32[]{:S(2)}) %collective-permute-start.11) | collective-permute-done | bytes 32032 | tf_op jit(solution)/shard_map/ppermute | solution.py:12
  91.3 2.0 collective-permute-start.12
  94.7 12.5 %collective-permute-start.14 = (f32[125,64]{0,1:T(8,128)S(1)}, f32[125,64]{0,1:T(8,128)S(1)}, u32[]{:S(2)}, u32[]{:S(2)}) collective-permute-start(f32[125,64]{0,1:T(8,128)S(1)} %select_bitcast_fusion.17), channel_id=1, source_target_pairs={{0,1},{1,2},{2,3},{4,5},{5,6},{6,7},{8,9},{9,10},{10,11},{12,13},{... | collective-permute-start | bytes 96008 | tf_op jit(solution)/shard_map/ppermute | solution.py:12
  108.9 4.3 %collective-permute-done.15 = f32[125,64]{0,1:T(8,128)S(1)} collective-permute-done((f32[125,64]{0,1:T(8,128)S(1)}, f32[125,64]{0,1:T(8,128)S(1)}, u32[]{:S(2)}, u32[]{:S(2)}) %collective-permute-start.15) | collective-permute-done | bytes 32032 | tf_op jit(solution)/shard_map/ppermute | solution.py:12
  113.2 1.5 conditional.11
  118.0 5.1 %collective-permute-start.16 = (f32[125,64]{0,1:T(8,128)S(1)}, f32[125,64]{0,1:T(8,128)S(1)}, u32[]{:S(2)}, u32[]{:S(2)}) collective-permute-start(f32[125,64]{0,1:T(8,128)S(1)} %select_bitcast_fusion.15), channel_id=1, source_target_pairs={{0,4},{4,8},{8,12},{12,16},{16,20},{20,24},{24,28},{1,5},{5,9},{9,... | collective-permute-start | bytes 96008 | tf_op jit(solution)/shard_map/ppermute | solution.py:12
  124.6 11.4 %collective-permute-start.18 = (f32[125,64]{0,1:T(8,128)S(1)}, f32[125,64]{0,1:T(8,128)S(1)}, u32[]{:S(2)}, u32[]{:S(2)}) collective-permute-start(f32[125,64]{0,1:T(8,128)S(1)} %select_bitcast_fusion.13), channel_id=1, source_target_pairs={{0,1},{1,2},{2,3},{4,5},{5,6},{6,7},{8,9},{9,10},{10,11},{12,13},{... | collective-permute-start | bytes 96008 | tf_op jit(solution)/shard_map/ppermute | solution.py:12
  137.6 4.5 %collective-permute-done.19 = f32[125,64]{0,1:T(8,128)S(1)} collective-permute-done((f32[125,64]{0,1:T(8,128)S(1)}, f32[125,64]{0,1:T(8,128)S(1)}, u32[]{:S(2)}, u32[]{:S(2)}) %collective-permute-start.19) | collective-permute-done | bytes 32032 | tf_op jit(solution)/shard_map/ppermute | solution.py:12
  142.1 10.7 %conditional.12 = (f32[125,128]{1,0:T(8,128)}, f32[]{:T(128)}) conditional(s32[]{:T(128)} %bitcast.108, f32[125,128]{1,0:T(8,128)} %get-tuple-element.174, (f32[4,128]{1,0:T(4,128)}, s32[4,128]{1,0:T(4,128)}, f32[125,384]{0,1:T(8,128)S(1)}, f32[125,128]{0,1:T(8,128)S(1)}, bf16[125,125,128]{2,1,0:T(8,128)(2,1)}, ...), branch_computations={%region_12.15_spmd, %region_13.0_spmd} | conditional | flops 6263167 | bytes 5311764 | solution.py:51
  146.7 4.0 %multiply_reduce_fusion.7 = f32[128,125]{0,1:T(8,128)} fusion(f32[128,125]{0,1:T(8,128)S(1)} %copy.99, bf16[125,125,128]{2,1,0:T(8,128)(2,1)} %get-tuple-element.131), kind=kLoop, calls=%fused_computation.177 | loop fusion | flops 5984000 | bytes 4128000 | tf_op jit(solution)/shard_map/cond/branch_1_fun/ijf,jf->if/dot_general | solution.py:40
  150.7 1.5 multiply_reduce_fusion.8
  161.7 2.8 %collective-permute-done.21 = f32[125,64]{0,1:T(8,128)S(1)} collective-permute-done((f32[125,64]{0,1:T(8,128)S(1)}, f32[125,64]{0,1:T(8,128)S(1)}, u32[]{:S(2)}, u32[]{:S(2)}) %collective-permute-start.21) | collective-permute-done | bytes 32032 | tf_op jit(solution)/shard_map/ppermute | solution.py:12
  164.5 1.7 collective-permute-done.23
  166.2 1.5 conditional.13
  171.0 15.0 %collective-permute-start.24 = (f32[125,64]{0,1:T(8,128)S(1)}, f32[125,64]{0,1:T(8,128)S(1)}, u32[]{:S(2)}, u32[]{:S(2)}) collective-permute-start(f32[125,64]{0,1:T(8,128)S(1)} %select_bitcast_fusion.7), channel_id=1, source_target_pairs={{0,4},{4,8},{8,12},{12,16},{16,20},{20,24},{24,28},{1,5},{5,9},{9,... | collective-permute-start | bytes 96008 | tf_op jit(solution)/shard_map/ppermute | solution.py:12
  190.3 4.5 %collective-permute-done.27 = f32[125,64]{0,1:T(8,128)S(1)} collective-permute-done((f32[125,64]{0,1:T(8,128)S(1)}, f32[125,64]{0,1:T(8,128)S(1)}, u32[]{:S(2)}, u32[]{:S(2)}) %collective-permute-start.27) | collective-permute-done | bytes 32032 | tf_op jit(solution)/shard_map/ppermute | solution.py:12
  199.7 2.0 collective-permute-start.28
  203.1 11.4 %collective-permute-start.30 = (f32[125,64]{0,1:T(8,128)S(1)}, f32[125,64]{0,1:T(8,128)S(1)}, u32[]{:S(2)}, u32[]{:S(2)}) collective-permute-start(f32[125,64]{0,1:T(8,128)S(1)} %select_bitcast_fusion.1), channel_id=1, source_target_pairs={{0,1},{1,2},{2,3},{4,5},{5,6},{6,7},{8,9},{9,10},{10,11},{12,13},{... | collective-permute-start | bytes 96008 | tf_op jit(solution)/shard_map/ppermute | solution.py:12
  216.2 4.3 %collective-permute-done.31 = f32[125,64]{0,1:T(8,128)S(1)} collective-permute-done((f32[125,64]{0,1:T(8,128)S(1)}, f32[125,64]{0,1:T(8,128)S(1)}, u32[]{:S(2)}, u32[]{:S(2)}) %collective-permute-start.31) | collective-permute-done | bytes 32032 | tf_op jit(solution)/shard_map/ppermute | solution.py:12
  222.0 51.8 %psum.7 = f32[2]{0:T(128)S(1)} all-reduce(f32[2]{0:T(128)S(1)} %pad_maximum_fusion), channel_id=1, replica_groups=mesh['gx'=8,'gy'=4] {'gx','gy'}, use_global_device_ids=true, to_apply=%region_24.27 | all-reduce | flops 2 | bytes 16 | tf_op jit(solution)/shard_map/psum | solution.py:56
  274.3 1.5 broadcast_in_dim.28
  (191 shorter events, 83.7 us)
Async XLA Ops:
  2.2 13.0 %collective-permute-start = (f32[125,64]{0,1:T(8,128)S(1)}, f32[125,64]{0,1:T(8,128)S(1)}, u32[]{:S(2)}, u32[]{:S(2)}) collective-permute-start(f32[125,64]{0,1:T(8,128)S(1)} %select_bitcast_fusion.31), channel_id=1, source_target_pairs={{0,4},{4,8},{8,12},{12,16},{16,20},{20,24},{24,28},{1,5},{5,9},{9,... | collective-permute-start | bytes 96008 | tf_op jit(solution)/shard_map/ppermute | solution.py:12
  5.3 9.9 %collective-permute-start.1 = (f32[125,64]{0,1:T(8,128)S(1)}, f32[125,64]{0,1:T(8,128)S(1)}, u32[]{:S(2)}, u32[]{:S(2)}) collective-permute-start(f32[125,64]{0,1:T(8,128)S(1)} %select_bitcast_fusion.30), channel_id=1, source_target_pairs={{4,0},{8,4},{12,8},{16,12},{20,16},{24,20},{28,24},{5,1},{9,5},{13... | collective-permute-start | bytes 96008 | tf_op jit(solution)/shard_map/ppermute | solution.py:12
  7.2 7.9 %collective-permute-start.2 = (f32[125,64]{0,1:T(8,128)S(1)}, f32[125,64]{0,1:T(8,128)S(1)}, u32[]{:S(2)}, u32[]{:S(2)}) collective-permute-start(f32[125,64]{0,1:T(8,128)S(1)} %select_bitcast_fusion.29), channel_id=1, source_target_pairs={{0,1},{1,2},{2,3},{4,5},{5,6},{6,7},{8,9},{9,10},{10,11},{12,13},{... | collective-permute-start | bytes 96008 | tf_op jit(solution)/shard_map/ppermute | solution.py:12
  12.2 5.8 %collective-permute-start.3 = (f32[125,64]{0,1:T(8,128)S(1)}, f32[125,64]{0,1:T(8,128)S(1)}, u32[]{:S(2)}, u32[]{:S(2)}) collective-permute-start(f32[125,64]{0,1:T(8,128)S(1)} %select_bitcast_fusion.28), channel_id=1, source_target_pairs={{1,0},{2,1},{3,2},{5,4},{6,5},{7,6},{9,8},{10,9},{11,10},{13,12},{... | collective-permute-start | bytes 96008 | tf_op jit(solution)/shard_map/ppermute | solution.py:12
  44.1 5.4 %collective-permute-start.4 = (f32[125,64]{0,1:T(8,128)S(1)}, f32[125,64]{0,1:T(8,128)S(1)}, u32[]{:S(2)}, u32[]{:S(2)}) collective-permute-start(f32[125,64]{0,1:T(8,128)S(1)} %select_bitcast_fusion.27), channel_id=1, source_target_pairs={{0,4},{4,8},{8,12},{12,16},{16,20},{20,24},{24,28},{1,5},{5,9},{9,... | collective-permute-start | bytes 96008 | tf_op jit(solution)/shard_map/ppermute | solution.py:12
  45.5 7.3 %collective-permute-start.5 = (f32[125,64]{0,1:T(8,128)S(1)}, f32[125,64]{0,1:T(8,128)S(1)}, u32[]{:S(2)}, u32[]{:S(2)}) collective-permute-start(f32[125,64]{0,1:T(8,128)S(1)} %select_bitcast_fusion.26), channel_id=1, source_target_pairs={{4,0},{8,4},{12,8},{16,12},{20,16},{24,20},{28,24},{5,1},{9,5},{13... | collective-permute-start | bytes 96008 | tf_op jit(solution)/shard_map/ppermute | solution.py:12
  46.9 6.0 %collective-permute-start.6 = (f32[125,64]{0,1:T(8,128)S(1)}, f32[125,64]{0,1:T(8,128)S(1)}, u32[]{:S(2)}, u32[]{:S(2)}) collective-permute-start(f32[125,64]{0,1:T(8,128)S(1)} %select_bitcast_fusion.25), channel_id=1, source_target_pairs={{0,1},{1,2},{2,3},{4,5},{5,6},{6,7},{8,9},{9,10},{10,11},{12,13},{... | collective-permute-start | bytes 96008 | tf_op jit(solution)/shard_map/ppermute | solution.py:12
  48.2 7.6 %collective-permute-start.7 = (f32[125,64]{0,1:T(8,128)S(1)}, f32[125,64]{0,1:T(8,128)S(1)}, u32[]{:S(2)}, u32[]{:S(2)}) collective-permute-start(f32[125,64]{0,1:T(8,128)S(1)} %select_bitcast_fusion.24), channel_id=1, source_target_pairs={{1,0},{2,1},{3,2},{5,4},{6,5},{7,6},{9,8},{10,9},{11,10},{13,12},{... | collective-permute-start | bytes 96008 | tf_op jit(solution)/shard_map/ppermute | solution.py:12
  59.2 21.9 %collective-permute-start.8 = (f32[125,64]{0,1:T(8,128)S(1)}, f32[125,64]{0,1:T(8,128)S(1)}, u32[]{:S(2)}, u32[]{:S(2)}) collective-permute-start(f32[125,64]{0,1:T(8,128)S(1)} %select_bitcast_fusion.23), channel_id=1, source_target_pairs={{0,4},{4,8},{8,12},{12,16},{16,20},{20,24},{24,28},{1,5},{5,9},{9,... | collective-permute-start | bytes 96008 | tf_op jit(solution)/shard_map/ppermute | solution.py:12
  77.0 4.1 %collective-permute-start.9 = (f32[125,64]{0,1:T(8,128)S(1)}, f32[125,64]{0,1:T(8,128)S(1)}, u32[]{:S(2)}, u32[]{:S(2)}) collective-permute-start(f32[125,64]{0,1:T(8,128)S(1)} %select_bitcast_fusion.22), channel_id=1, source_target_pairs={{4,0},{8,4},{12,8},{16,12},{20,16},{24,20},{28,24},{5,1},{9,5},{13... | collective-permute-start | bytes 96008 | tf_op jit(solution)/shard_map/ppermute | solution.py:12
  78.4 2.9 %collective-permute-start.10 = (f32[125,64]{0,1:T(8,128)S(1)}, f32[125,64]{0,1:T(8,128)S(1)}, u32[]{:S(2)}, u32[]{:S(2)}) collective-permute-start(f32[125,64]{0,1:T(8,128)S(1)} %select_bitcast_fusion.21), channel_id=1, source_target_pairs={{0,1},{1,2},{2,3},{4,5},{5,6},{6,7},{8,9},{9,10},{10,11},{12,13},{... | collective-permute-start | bytes 96008 | tf_op jit(solution)/shard_map/ppermute | solution.py:12
  79.8 6.6 %collective-permute-start.11 = (f32[125,64]{0,1:T(8,128)S(1)}, f32[125,64]{0,1:T(8,128)S(1)}, u32[]{:S(2)}, u32[]{:S(2)}) collective-permute-start(f32[125,64]{0,1:T(8,128)S(1)} %select_bitcast_fusion.20), channel_id=1, source_target_pairs={{1,0},{2,1},{3,2},{5,4},{6,5},{7,6},{9,8},{10,9},{11,10},{13,12},{... | collective-permute-start | bytes 96008 | tf_op jit(solution)/shard_map/ppermute | solution.py:12
  91.3 17.4 %collective-permute-start.12 = (f32[125,64]{0,1:T(8,128)S(1)}, f32[125,64]{0,1:T(8,128)S(1)}, u32[]{:S(2)}, u32[]{:S(2)}) collective-permute-start(f32[125,64]{0,1:T(8,128)S(1)} %select_bitcast_fusion.19), channel_id=1, source_target_pairs={{0,4},{4,8},{8,12},{12,16},{16,20},{20,24},{24,28},{1,5},{5,9},{9,... | collective-permute-start | bytes 96008 | tf_op jit(solution)/shard_map/ppermute | solution.py:12
  93.4 15.3 %collective-permute-start.13 = (f32[125,64]{0,1:T(8,128)S(1)}, f32[125,64]{0,1:T(8,128)S(1)}, u32[]{:S(2)}, u32[]{:S(2)}) collective-permute-start(f32[125,64]{0,1:T(8,128)S(1)} %select_bitcast_fusion.18), channel_id=1, source_target_pairs={{4,0},{8,4},{12,8},{16,12},{20,16},{24,20},{28,24},{5,1},{9,5},{13... | collective-permute-start | bytes 96008 | tf_op jit(solution)/shard_map/ppermute | solution.py:12
  94.7 14.1 %collective-permute-start.14 = (f32[125,64]{0,1:T(8,128)S(1)}, f32[125,64]{0,1:T(8,128)S(1)}, u32[]{:S(2)}, u32[]{:S(2)}) collective-permute-start(f32[125,64]{0,1:T(8,128)S(1)} %select_bitcast_fusion.17), channel_id=1, source_target_pairs={{0,1},{1,2},{2,3},{4,5},{5,6},{6,7},{8,9},{9,10},{10,11},{12,13},{... | collective-permute-start | bytes 96008 | tf_op jit(solution)/shard_map/ppermute | solution.py:12
  107.4 5.8 %collective-permute-start.15 = (f32[125,64]{0,1:T(8,128)S(1)}, f32[125,64]{0,1:T(8,128)S(1)}, u32[]{:S(2)}, u32[]{:S(2)}) collective-permute-start(f32[125,64]{0,1:T(8,128)S(1)} %select_bitcast_fusion.16), channel_id=1, source_target_pairs={{1,0},{2,1},{3,2},{5,4},{6,5},{7,6},{9,8},{10,9},{11,10},{13,12},{... | collective-permute-start | bytes 96008 | tf_op jit(solution)/shard_map/ppermute | solution.py:12
  118.0 19.3 %collective-permute-start.16 = (f32[125,64]{0,1:T(8,128)S(1)}, f32[125,64]{0,1:T(8,128)S(1)}, u32[]{:S(2)}, u32[]{:S(2)}) collective-permute-start(f32[125,64]{0,1:T(8,128)S(1)} %select_bitcast_fusion.15), channel_id=1, source_target_pairs={{0,4},{4,8},{8,12},{12,16},{16,20},{20,24},{24,28},{1,5},{5,9},{9,... | collective-permute-start | bytes 96008 | tf_op jit(solution)/shard_map/ppermute | solution.py:12
  123.2 14.2 %collective-permute-start.17 = (f32[125,64]{0,1:T(8,128)S(1)}, f32[125,64]{0,1:T(8,128)S(1)}, u32[]{:S(2)}, u32[]{:S(2)}) collective-permute-start(f32[125,64]{0,1:T(8,128)S(1)} %select_bitcast_fusion.14), channel_id=1, source_target_pairs={{4,0},{8,4},{12,8},{16,12},{20,16},{24,20},{28,24},{5,1},{9,5},{13... | collective-permute-start | bytes 96008 | tf_op jit(solution)/shard_map/ppermute | solution.py:12
  124.6 13.1 %collective-permute-start.18 = (f32[125,64]{0,1:T(8,128)S(1)}, f32[125,64]{0,1:T(8,128)S(1)}, u32[]{:S(2)}, u32[]{:S(2)}) collective-permute-start(f32[125,64]{0,1:T(8,128)S(1)} %select_bitcast_fusion.13), channel_id=1, source_target_pairs={{0,1},{1,2},{2,3},{4,5},{5,6},{6,7},{8,9},{9,10},{10,11},{12,13},{... | collective-permute-start | bytes 96008 | tf_op jit(solution)/shard_map/ppermute | solution.py:12
  136.1 6.0 %collective-permute-start.19 = (f32[125,64]{0,1:T(8,128)S(1)}, f32[125,64]{0,1:T(8,128)S(1)}, u32[]{:S(2)}, u32[]{:S(2)}) collective-permute-start(f32[125,64]{0,1:T(8,128)S(1)} %select_bitcast_fusion.12), channel_id=1, source_target_pairs={{1,0},{2,1},{3,2},{5,4},{6,5},{7,6},{9,8},{10,9},{11,10},{13,12},{... | collective-permute-start | bytes 96008 | tf_op jit(solution)/shard_map/ppermute | solution.py:12
  156.2 5.4 %collective-permute-start.20 = (f32[125,64]{0,1:T(8,128)S(1)}, f32[125,64]{0,1:T(8,128)S(1)}, u32[]{:S(2)}, u32[]{:S(2)}) collective-permute-start(f32[125,64]{0,1:T(8,128)S(1)} %select_bitcast_fusion.11), channel_id=1, source_target_pairs={{0,4},{4,8},{8,12},{12,16},{16,20},{20,24},{24,28},{1,5},{5,9},{9,... | collective-permute-start | bytes 96008 | tf_op jit(solution)/shard_map/ppermute | solution.py:12
  157.6 6.8 %collective-permute-start.21 = (f32[125,64]{0,1:T(8,128)S(1)}, f32[125,64]{0,1:T(8,128)S(1)}, u32[]{:S(2)}, u32[]{:S(2)}) collective-permute-start(f32[125,64]{0,1:T(8,128)S(1)} %select_bitcast_fusion.10), channel_id=1, source_target_pairs={{4,0},{8,4},{12,8},{16,12},{20,16},{24,20},{28,24},{5,1},{9,5},{13... | collective-permute-start | bytes 96008 | tf_op jit(solution)/shard_map/ppermute | solution.py:12
  159.0 5.5 %collective-permute-start.22 = (f32[125,64]{0,1:T(8,128)S(1)}, f32[125,64]{0,1:T(8,128)S(1)}, u32[]{:S(2)}, u32[]{:S(2)}) collective-permute-start(f32[125,64]{0,1:T(8,128)S(1)} %select_bitcast_fusion.9), channel_id=1, source_target_pairs={{0,1},{1,2},{2,3},{4,5},{5,6},{6,7},{8,9},{9,10},{10,11},{12,13},{... | collective-permute-start | bytes 96008 | tf_op jit(solution)/shard_map/ppermute | solution.py:12
  160.3 5.8 %collective-permute-start.23 = (f32[125,64]{0,1:T(8,128)S(1)}, f32[125,64]{0,1:T(8,128)S(1)}, u32[]{:S(2)}, u32[]{:S(2)}) collective-permute-start(f32[125,64]{0,1:T(8,128)S(1)} %select_bitcast_fusion.8), channel_id=1, source_target_pairs={{1,0},{2,1},{3,2},{5,4},{6,5},{7,6},{9,8},{10,9},{11,10},{13,12},{... | collective-permute-start | bytes 96008 | tf_op jit(solution)/shard_map/ppermute | solution.py:12
  171.0 19.1 %collective-permute-start.24 = (f32[125,64]{0,1:T(8,128)S(1)}, f32[125,64]{0,1:T(8,128)S(1)}, u32[]{:S(2)}, u32[]{:S(2)}) collective-permute-start(f32[125,64]{0,1:T(8,128)S(1)} %select_bitcast_fusion.7), channel_id=1, source_target_pairs={{0,4},{4,8},{8,12},{12,16},{16,20},{20,24},{24,28},{1,5},{5,9},{9,... | collective-permute-start | bytes 96008 | tf_op jit(solution)/shard_map/ppermute | solution.py:12
  186.1 4.1 %collective-permute-start.25 = (f32[125,64]{0,1:T(8,128)S(1)}, f32[125,64]{0,1:T(8,128)S(1)}, u32[]{:S(2)}, u32[]{:S(2)}) collective-permute-start(f32[125,64]{0,1:T(8,128)S(1)} %select_bitcast_fusion.6), channel_id=1, source_target_pairs={{4,0},{8,4},{12,8},{16,12},{20,16},{24,20},{28,24},{5,1},{9,5},{13... | collective-permute-start | bytes 96008 | tf_op jit(solution)/shard_map/ppermute | solution.py:12
  187.4 2.9 %collective-permute-start.26 = (f32[125,64]{0,1:T(8,128)S(1)}, f32[125,64]{0,1:T(8,128)S(1)}, u32[]{:S(2)}, u32[]{:S(2)}) collective-permute-start(f32[125,64]{0,1:T(8,128)S(1)} %select_bitcast_fusion.5), channel_id=1, source_target_pairs={{0,1},{1,2},{2,3},{4,5},{5,6},{6,7},{8,9},{9,10},{10,11},{12,13},{... | collective-permute-start | bytes 96008 | tf_op jit(solution)/shard_map/ppermute | solution.py:12
  188.8 6.0 %collective-permute-start.27 = (f32[125,64]{0,1:T(8,128)S(1)}, f32[125,64]{0,1:T(8,128)S(1)}, u32[]{:S(2)}, u32[]{:S(2)}) collective-permute-start(f32[125,64]{0,1:T(8,128)S(1)} %select_bitcast_fusion.4), channel_id=1, source_target_pairs={{1,0},{2,1},{3,2},{5,4},{6,5},{7,6},{9,8},{10,9},{11,10},{13,12},{... | collective-permute-start | bytes 96008 | tf_op jit(solution)/shard_map/ppermute | solution.py:12
  199.7 16.3 %collective-permute-start.28 = (f32[125,64]{0,1:T(8,128)S(1)}, f32[125,64]{0,1:T(8,128)S(1)}, u32[]{:S(2)}, u32[]{:S(2)}) collective-permute-start(f32[125,64]{0,1:T(8,128)S(1)} %select_bitcast_fusion.3), channel_id=1, source_target_pairs={{0,4},{4,8},{8,12},{12,16},{16,20},{20,24},{24,28},{1,5},{5,9},{9,... | collective-permute-start | bytes 96008 | tf_op jit(solution)/shard_map/ppermute | solution.py:12
  201.8 14.2 %collective-permute-start.29 = (f32[125,64]{0,1:T(8,128)S(1)}, f32[125,64]{0,1:T(8,128)S(1)}, u32[]{:S(2)}, u32[]{:S(2)}) collective-permute-start(f32[125,64]{0,1:T(8,128)S(1)} %select_bitcast_fusion.2), channel_id=1, source_target_pairs={{4,0},{8,4},{12,8},{16,12},{20,16},{24,20},{28,24},{5,1},{9,5},{13... | collective-permute-start | bytes 96008 | tf_op jit(solution)/shard_map/ppermute | solution.py:12
  203.1 13.0 %collective-permute-start.30 = (f32[125,64]{0,1:T(8,128)S(1)}, f32[125,64]{0,1:T(8,128)S(1)}, u32[]{:S(2)}, u32[]{:S(2)}) collective-permute-start(f32[125,64]{0,1:T(8,128)S(1)} %select_bitcast_fusion.1), channel_id=1, source_target_pairs={{0,1},{1,2},{2,3},{4,5},{5,6},{6,7},{8,9},{9,10},{10,11},{12,13},{... | collective-permute-start | bytes 96008 | tf_op jit(solution)/shard_map/ppermute | solution.py:12
  214.6 5.8 %collective-permute-start.31 = (f32[125,64]{0,1:T(8,128)S(1)}, f32[125,64]{0,1:T(8,128)S(1)}, u32[]{:S(2)}, u32[]{:S(2)}) collective-permute-start(f32[125,64]{0,1:T(8,128)S(1)} %select_bitcast_fusion), channel_id=1, source_target_pairs={{1,0},{2,1},{3,2},{5,4},{6,5},{7,6},{9,8},{10,9},{11,10},{13,12},{... | collective-permute-start | bytes 96008 | tf_op jit(solution)/shard_map/ppermute | solution.py:12
where the time goes:
time: 275 us; the launch traced here: 276 us
  starting transfers between devices  112 us (41%)
  local copies, waits for them, and re-layouts  55 us (20%)
  blocking collectives  51.8 us (19%)
  waiting for transfers between devices  37.1 us (13%)
  other arithmetic  12.5 us (5%)
  matrix products  4 us (1%)
    ppermute x32, starting transfers between devices, from_behind(): lax.ppermute(value, axis, [(source, source + steps) for source in range(l...  112 us
    psum x1, blocking collectives, body(): totals = lax.psum(jnp.stack(locals_list), ('gx', 'gy'))  51.8 us
    ppermute x32, waiting for transfers between devices, from_behind(): lax.ppermute(value, axis, [(source, source + steps) for source in range(l...  37.1 us
    gather x32, local copies, waits for them, and re-layouts, gather_margin(): packs = [jnp.take(solution, sending[side], axis=1) for side in range(4)]  22.4 us
    cond x6, local copies, waits for them, and re-layouts  7.41 us
    another operation x1, local copies, waits for them, and re-layouts  7.16 us
    cond x7, local copies, waits for them, and re-layouts, body(): lax.cond(own_color == color, update, unchanged, (extended, solution))  7.13 us
  transfers between devices with their start and end apart: 32, of which 15 were waited for; matrix products, arithmetic and copies ran while one was open for 2% of the time, Pallas kernels for 0%

commit v1 on v0

v1 whole, which is shorter than its diff:
```python
import jax
import jax.numpy as jnp
from jax import lax
from jax.experimental import pallas as pl
from jax.experimental.pallas import tpu as pltpu
from jax.sharding import PartitionSpec as P

LANES = 128
SUB = 8
GROUP = 25
VMEM_LIMIT = 16 * 1024 * 1024
CHUNKS = 5
HELD = 3
FIRST, SECOND, CONTROL = range(3)

VSPEC = pl.BlockSpec(memory_space=pltpu.VMEM)
SSPEC = pl.BlockSpec(memory_space=pltpu.SMEM)


def vmem(value):
    return pltpu.with_memory_space_constraint(value, pltpu.VMEM)


def hbm(value):
    return pltpu.with_memory_space_constraint(value, pltpu.HBM)


def smem(value):
    return pltpu.with_memory_space_constraint(value, pltpu.SMEM)


class Plan:
    def __init__(self, mesh, rows, faces, halo, neigh):
        self.nx, self.ny = mesh.shape["gx"], mesh.shape["gy"]
        self.rows, self.faces, self.halo, self.neigh = rows, faces, halo, neigh
        assert self.nx % 2 == 0 and self.ny % 2 == 0
        assert faces == LANES and 2 * halo == LANES
        self.tiles = -(-rows // (2 * SUB)) * 2
        self.pad = self.tiles * SUB
        self.half = self.pad // 2
        assert rows % CHUNKS == 0
        self.chunk = rows // CHUNKS
        self.along = (self.pad, 2 * self.pad)
        self.rhs = 3 * self.pad
        self.norm = 4 * self.pad
        self.step = self.norm + 2 * SUB
        self.state = self.step + SUB
        self.state_type = pltpu.VMEM((self.state, LANES), jnp.float32)
        self.pack_type = pltpu.VMEM((self.half, LANES), jnp.float32)
        self.control_type = pltpu.SMEM((CONTROL,), jnp.int32)

    def held_type(self, inverse):
        return pltpu.VMEM((HELD * self.chunk, *inverse.shape[1:]), inverse.dtype)

    def rest_type(self, inverse):
        return pltpu.VMEM(((CHUNKS - HELD) * self.chunk, *inverse.shape[1:]), inverse.dtype)


def write_pack(plan, state, lists, row, ref):
    low = lax.broadcasted_iota(jnp.int32, (SUB, LANES), 1) < plan.halo
    index = jnp.broadcast_to(lists[pl.ds(row, 1), :], (SUB, LANES))

    def take(t):
        tile = state[t * SUB:(t + 1) * SUB, :]
        return jnp.take_along_axis(tile, index, axis=1, mode="promise_in_bounds")

    for t in range(plan.tiles // 2):
        ref[t * SUB:(t + 1) * SUB, :] = jnp.where(low, take(t), take(t + plan.tiles // 2))


def merge(plan, state, base, even, odd):
    low = lax.broadcasted_iota(jnp.int32, (SUB, LANES), 1) < plan.halo
    for t in range(plan.tiles // 2):
        a = even[t * SUB:(t + 1) * SUB, :]
        b = odd[t * SUB:(t + 1) * SUB, :]
        first = jnp.where(low, a, pltpu.roll(b, plan.halo, 1))
        second = jnp.where(low, pltpu.roll(a, plan.halo, 1), b)
        state[pl.ds(base + t * SUB, SUB), :] = first
        state[pl.ds(base + plan.half + t * SUB, SUB), :] = second


def apply_inverse(plan, blocks, source, result, base, start, stop):
    src = source[0:plan.rows, :]
    group = max(g for g in range(1, GROUP + 1) if (stop - start) % g == 0)

    def step(n, carry):
        for k in range(group):
            i = start + n * group + k
            block = blocks[i].astype(jnp.float32)
            result[pl.ds(base + i, 1), :] = jnp.sum(block * src, axis=0, keepdims=True)
        return carry

    lax.fori_loop(0, (stop - start) // group, step, 0)


def chunk_copies(plan, inverse, kept, rest, sems, first):
    copies = []
    for n in range(first, CHUNKS):
        part = inverse.at[pl.ds(n * plan.chunk, plan.chunk)]
        ref, at = (kept, n) if n < HELD else (rest, n - HELD)
        copies.append(pltpu.make_async_copy(part, ref.at[pl.ds(at * plan.chunk, plan.chunk)], sems.at[n]))
    return copies


def apply_chunks(plan, kept, rest, source, result, start, stop):
    held = HELD * plan.chunk
    if start < HELD:
        apply_inverse(plan, kept, source, result, 0, start * plan.chunk, min(stop, HELD) * plan.chunk)
    if stop > HELD:
        apply_inverse(plan, rest, source, result, held, max(start - HELD, 0) * plan.chunk, (stop - HELD) * plan.chunk)


def parts_of(value):
    high = value.astype(jnp.bfloat16)
    low = (value - high.astype(jnp.float32)).astype(jnp.bfloat16)
    return high, low


def update(plan, second, state, coupling, inverse, kept, rest, source, result, sems):
    copies = chunk_copies(plan, inverse, kept, rest, sems, HELD)
    for c in copies:
        c.start()
    pad = plan.pad
    values = jnp.concatenate([state[n * pad:(n + 1) * pad, :] for n in range(3)], axis=1)
    high, low = parts_of(values)
    size = 3 * LANES
    couple = jnp.dot(high, coupling[0:size, :], preferred_element_type=jnp.float32)
    couple = couple + jnp.dot(low, coupling[0:size, :], preferred_element_type=jnp.float32)
    couple = couple + jnp.dot(high, coupling[size:2 * size, :], preferred_element_type=jnp.float32)
    right = state[plan.rhs:plan.rhs + pad, :]
    source[...] = (right + couple).astype(jnp.bfloat16).astype(jnp.float32)
    result[pad - SUB:pad, :] = jnp.zeros((SUB, LANES), jnp.float32)
    apply_chunks(plan, kept, rest, source, result, 0, HELD)
    for c in copies:
        c.wait()
    apply_chunks(plan, kept, rest, source, result, HELD, CHUNKS)
    finish(plan, second, state, result)


def finish(plan, second, state, result):
    squares = jnp.zeros((SUB, LANES), jnp.float32)
    for t in range(plan.tiles):
        new = result[t * SUB:(t + 1) * SUB, :]
        delta = new - state[t * SUB:(t + 1) * SUB, :]
        squares = squares + delta * delta
        state[t * SUB:(t + 1) * SUB, :] = new
    state[pl.ds(pl.multiple_of(plan.norm + second * SUB, SUB), SUB), :] = squares


def first_kernel(plan):
    rows, pad, neigh = plan.rows, plan.pad, plan.neigh

    def kernel(color, color_x, color_y, rhs, weights, neighbours, lists, inverse,
               code, control, kept, state, coupling, table, xe, xo, ye, yo,
               cx, cy, rhs_v, weights_v, slots_v, lists_v, rest, source, result, sems, part_sems):
        moves = ((color_x, cx), (color_y, cy), (neighbours, slots_v), (weights, weights_v),
                 (lists, lists_v), (rhs, rhs_v))
        copies = [pltpu.make_async_copy(a, b, sems.at[n]) for n, (a, b) in enumerate(moves)]
        parts = chunk_copies(plan, inverse, kept, rest, part_sems, 0)
        for c in copies + parts:
            c.start()
        odd_x = lax.axis_index("gx") & 1
        odd_y = lax.axis_index("gy") & 1
        state[...] = jnp.zeros(state.shape, jnp.float32)
        for c in copies[:2]:
            c.wait()
        mine, beside_x, beside_y = color[0, 0], cx[0, 0], cy[0, 0]
        across = 6 - mine - beside_x - beside_y
        to_x = jnp.logical_or(beside_x == 0, across == 0).astype(jnp.int32)
        to_y = jnp.logical_or(beside_y == 0, across == 0).astype(jnp.int32)
        zero_x, zero_y = odd_x ^ to_x, odd_y ^ to_y
        opposite = jnp.where(to_x == 0, jnp.where(to_y == 0, across, beside_x), jnp.where(to_y == 0, beside_y, mine))
        next_x = jnp.where(to_x == 0, jnp.where(to_y == 0, beside_x, across), jnp.where(to_y == 0, mine, beside_y))
        chain = opposite == 2
        first = jnp.where(chain, mine, jnp.where(opposite == 1, mine >> 1, (mine + 1) >> 1))
        control[FIRST] = first
        control[SECOND] = first + jnp.where(chain, 4, 2)
        red = zero_x ^ zero_y
        total = 0
        for n in range(7):
            step = n >> 1 & 1
            alternate = jnp.where(n < jnp.where(opposite == 1, 3, 4), 5 + (red ^ (n & 1)), 0)
            axis_x = 1 + 2 * (zero_x ^ step)
            axis_y = 2 + 2 * (zero_y ^ step)
            around = jnp.where((next_x == 1) == (n % 2 == 0), axis_x, axis_y)
            total = total + (jnp.where(chain, around, alternate) << (4 * n))
        code[0] = total

        for c in copies[2:]:
            c.wait()
        state[plan.rhs:plan.rhs + rows, :] = rhs_v[:, 0, :]
        source[...] = state[plan.rhs:plan.rhs + pad, :].astype(jnp.bfloat16).astype(jnp.float32)

        slots = slots_v[...]
        group = (slots - plan.faces) // plan.halo
        within = (slots - plan.faces) & (plan.halo - 1)
        along_y = (group >= 2).astype(jnp.int32)
        side = ((group & 1) + 1 + jnp.where(group >= 2, odd_y, odd_x)) & 1
        place = jnp.where(slots < plan.faces, slots, plan.faces * (1 + along_y) + within + plan.halo * side)
        size = 3 * LANES
        where = lax.broadcasted_iota(jnp.int32, (size, LANES), 0)
        total = jnp.zeros((size, LANES), jnp.float32)
        for k in range(neigh):
            total = total + jnp.where(where == place[k:k + 1, :], weights_v[k:k + 1, :], 0.0)
        coupling[0:size, :], coupling[size:2 * size, :] = parts_of(total)

        both = jnp.concatenate([lists_v[...], lists_v[...]], axis=1)
        table[...] = jnp.zeros(table.shape, jnp.int32)
        for n, odd in ((0, odd_x), (2, odd_y)):
            table[n:n + 1, :] = jnp.where(odd == 0, both[n:n + 1], both[n + 1:n + 2])
            table[n + 1:n + 2, :] = jnp.where(odd == 0, both[n + 1:n + 2], both[n:n + 1])

        result[pad - SUB:pad, :] = jnp.zeros((SUB, LANES), jnp.float32)
        for n in range(CHUNKS):
            parts[n].wait()

            @pl.when(first == 0)
            def _():
                apply_chunks(plan, kept, rest, source, result, n, n + 1)

        @pl.when(first == 0)
        def _():
            finish(plan, 0, state, result)

        for n, ref in enumerate((xe, xo, ye, yo)):
            write_pack(plan, state, table, n, ref)

    def call(color, color_x, color_y, rhs, weights, neighbours, lists, inverse):
        return pl.pallas_call(
            kernel,
            name="first",
            in_specs=[SSPEC, pl.BlockSpec(memory_space=pl.ANY), pl.BlockSpec(memory_space=pl.ANY)]
            + [pl.BlockSpec(memory_space=pltpu.HBM)] * 5,
            out_specs=[SSPEC] * 2 + [VSPEC] * 8,
            out_shape=[
                pltpu.SMEM((1,), jnp.int32),
                plan.control_type,
                plan.held_type(inverse),
                plan.state_type,
                pltpu.VMEM((6 * LANES, LANES), jnp.bfloat16),
                pltpu.VMEM((SUB, LANES), jnp.int32),
            ] + [plan.pack_type] * 4,
            compiler_params=pltpu.CompilerParams(vmem_limit_bytes=VMEM_LIMIT),
            scratch_shapes=[
                pltpu.SMEM(color.shape, color.dtype),
                pltpu.SMEM(color.shape, color.dtype),
                pltpu.VMEM(rhs.shape, rhs.dtype),
                pltpu.VMEM(weights.shape, weights.dtype),
                pltpu.VMEM(neighbours.shape, neighbours.dtype),
                pltpu.VMEM(lists.shape, lists.dtype),
                plan.rest_type(inverse),
                pltpu.VMEM((pad, LANES), jnp.float32),
                pltpu.VMEM((pad, LANES), jnp.float32),
                pltpu.SemaphoreType.DMA((6,)),
                pltpu.SemaphoreType.DMA((CHUNKS,)),
            ],
        )(color, color_x, color_y, *(hbm(v) for v in (rhs, weights, neighbours, lists, inverse)))

    return call


def merge_kernel(plan, name, receives, axes):
    def kernel(*refs):
        old_state, *got = refs[:-1]
        state = refs[-1]
        del old_state
        odd_x = lax.axis_index("gx") & 1
        odd_y = lax.axis_index("gy") & 1

        @pl.when(receives(odd_x, odd_y))
        def _():
            for n, axis in enumerate(axes):
                merge(plan, state, plan.along[axis], got[2 * n], got[2 * n + 1])

    def call(state, got):
        return pl.pallas_call(
            kernel,
            name=name,
            in_specs=[VSPEC] * (1 + len(got)),
            out_specs=VSPEC,
            out_shape=plan.state_type,
            input_output_aliases={0: 0},
            compiler_params=pltpu.CompilerParams(vmem_limit_bytes=VMEM_LIMIT),
        )(*(vmem(v) for v in (state, *got)))

    return call


def level_kernel(plan):
    def kernel(control, old_state, coupling, table, kept, inverse, state, xe, xo, ye, yo, rest, source, result, sems):
        del old_state
        steps = state[plan.step:plan.step + SUB, :] + 1.0
        state[plan.step:plan.step + SUB, :] = steps
        step = steps[0, 0].astype(jnp.int32)
        second = (step == control[SECOND]).astype(jnp.int32)
        turn = jnp.logical_or(step == control[FIRST], step == control[SECOND])

        @pl.when(turn)
        def _():
            update(plan, second, state, coupling, inverse, kept, rest, source, result, sems)

        for n, ref in enumerate((xe, xo, ye, yo)):
            write_pack(plan, state, table, n, ref)

    def call(control, state, coupling, table, kept, inverse):
        return pl.pallas_call(
            kernel,
            name="level",
            in_specs=[SSPEC] + [VSPEC] * 4 + [pl.BlockSpec(memory_space=pltpu.HBM)],
            out_specs=[VSPEC] * 5,
            out_shape=[plan.state_type] + [plan.pack_type] * 4,
            input_output_aliases={1: 0},
            compiler_params=pltpu.CompilerParams(vmem_limit_bytes=VMEM_LIMIT),
            scratch_shapes=[
                plan.rest_type(inverse),
                pltpu.VMEM((plan.pad, LANES), jnp.float32),
                pltpu.VMEM((plan.pad, LANES), jnp.float32),
                pltpu.SemaphoreType.DMA((CHUNKS,)),
            ],
        )(smem(control), *(vmem(v) for v in (state, coupling, table, kept)), hbm(inverse))

    return call


def last_kernel(plan):
    devices = plan.nx * plan.ny

    def kernel(state, out, sums):
        out[:, 0, :] = state[0:plan.rows, :]
        lane = lax.broadcasted_iota(jnp.int32, (devices, LANES), 1)
        first = jnp.sum(state[plan.norm:plan.norm + SUB, :])
        second = jnp.sum(state[plan.norm + SUB:plan.norm + 2 * SUB, :])
        sums[...] = jnp.where(lane == 0, first, jnp.where(lane == 1, second, 0.0))

    def call(state):
        return pl.pallas_call(
            kernel,
            name="last",
            in_specs=[VSPEC],
            out_specs=[VSPEC] * 2,
            out_shape=[
                pltpu.VMEM((plan.rows, 1, LANES), jnp.float32),
                pltpu.VMEM((devices, LANES), jnp.float32),
            ],
            compiler_params=pltpu.CompilerParams(vmem_limit_bytes=VMEM_LIMIT),
        )(vmem(state))

    return call


def edge_pairs(plan, axis, odd, sends, both):
    pairs = []
    for i in range(plan.nx):
        for j in range(plan.ny):
            u, v = (i + 1, j) if axis == 0 else (i, j + 1)
            if (i, j)[axis] % 2 != odd or u >= plan.nx or v >= plan.ny:
                continue
            here, there = i * plan.ny + j, u * plan.ny + v
            if both or sends(i, j):
                pairs.append((here, there))
            if both or sends(u, v):
                pairs.append((there, here))
    return pairs


def flow(plan, name, axes, parity):
    steps = [(axis, odd) for axis in axes for odd in (0, 1)]

    def sends(i, j):
        return (i * (0 in axes) + j * (1 in axes)) % 2 == parity

    def receives(i, j):
        return ((i if axes == (0,) else j if axes == (1,) else i ^ j) & 1) != parity

    def run(state, *packs):
        got = []
        for n, (axis, odd) in enumerate(steps):
            pairs = edge_pairs(plan, axis, odd, sends, n == len(steps) - 1)
            got.append(lax.ppermute(packs[2 * axis + odd], ("gx", "gy"), pairs))
        return merge_kernel(plan, name, receives, axes)(state, got)

    return run


def body_for(mesh):
    def body(rhs, inverse, weights, neighbours, send_lists, coloring):
        rows, faces = rhs.shape[1:]
        plan = Plan(mesh, rows, faces, send_lists.shape[2], weights.shape[1])
        color_x = lax.ppermute(coloring, "gx", [(i, i ^ 1) for i in range(plan.nx)])
        color_y = lax.ppermute(coloring, "gy", [(j, j ^ 1) for j in range(plan.ny)])
        code, control, kept, state, coupling, table, *packs = first_kernel(plan)(
            coloring, color_x, color_y, rhs.transpose(1, 0, 2), weights[0], neighbours[0], send_lists[0], inverse[0])
        flows = [
            flow(plan, "along_x0", (0,), 0),
            flow(plan, "along_y0", (1,), 0),
            flow(plan, "along_x1", (0,), 1),
            flow(plan, "along_y1", (1,), 1),
            flow(plan, "both0", (0, 1), 0),
            flow(plan, "both1", (0, 1), 1),
        ]

        def turn(carry):
            code, state, packs = carry
            state = lax.switch((code & 7) - 1, flows, state, *packs)
            state, *packs = level_kernel(plan)(control, state, coupling, table, kept, inverse[0])
            return code >> 4, state, tuple(packs)

        state = lax.while_loop(lambda carry: carry[0] != 0, turn, (code[0], state, tuple(packs)))[1]
        out, sums = last_kernel(plan)(state)
        sums = lax.all_to_all(sums, ("gx", "gy"), 0, 0, tiled=True)
        norms = jnp.sqrt(jnp.sum(sums[:, :2], axis=0))
        return out.transpose(1, 0, 2), norms

    return body


def solution(mesh):
    in_specs = (
        P("gx", None, "gy"),
        P("gx", None, None, "gy"),
        P("gx", None, "gy"),
        P("gx", None, "gy"),
        P("gx", None, "gy"),
        P("gx", "gy"),
    )
    out_specs = (P("gx", None, "gy"), P())
    return jax.shard_map(body_for(mesh), mesh=mesh, in_specs=in_specs, out_specs=out_specs, check_vma=False)
```

time: 275 us -> 69.2 us (0.25)
  starting transfers between devices: 112 us -> 34.2 us
  local copies, waits for them, and re-layouts: 55 us -> 1.15 us
  blocking collectives: 51.8 us -> 0 us
  waiting for transfers between devices: 37.1 us -> 21.8 us
  other arithmetic: 12.5 us -> 0.02 us
  Pallas kernels: 0 us -> 9.3 us
  matrix products: 4 us -> 0 us
    ppermute x32 -> x18, starting transfers between devices: 112 us -> 24 us  [the longest x16 20.8 us: run(): got.append(lax.ppermute(packs[2 * axis + odd], ('gx', 'gy'), pairs))]
    psum x1 -> x0, blocking collectives: 51.8 us -> none  [body(): totals = lax.psum(jnp.stack(locals_list), ('gx', 'gy'))]
    gather x40 -> x0, local copies, waits for them, and re-layouts: 27.6 us -> none  [the longest x32 22.4 us: gather_margin(): packs = [jnp.take(solution, sending[side], axis=1) for side in range(4)]]
    ppermute x32 -> x18, waiting for transfers between devices: 37.1 us -> 15.2 us  [the longest x16 14.1 us: run(): got.append(lax.ppermute(packs[2 * axis + odd], ('gx', 'gy'), pairs))]
    cond x13 -> x0, local copies, waits for them, and re-layouts: 14.5 us -> none
    all_to_all x0 -> x1, starting transfers between devices: none -> 10.2 us  [body(): sums = lax.all_to_all(sums, ('gx', 'gy'), 0, 0, tiled=True)]
    pallas_call x0 -> x10, Pallas kernels: none -> 9.3 us  [the longest x4 4.68 us: call(): pl.pallas_call(kernel, name='level', in_specs=[SSPEC] + [VSPEC] * 4 + [pl...]
    another operation x1 -> x0, local copies, waits for them, and re-layouts: 7.16 us -> none
  transfers between devices with their start and end apart: 32 -> 19, of which waited for: 15 -> 7; matrix products, arithmetic and copies ran while one was open for 2% -> 1% of each run, Pallas kernels for 0% -> 0%
where the time goes in v1:
time: 69.2 us; the launch traced here: 68.5 us
  starting transfers between devices  34.2 us (49%)
  waiting for transfers between devices  21.8 us (32%)
  Pallas kernels  9.3 us (13%)
  between operations  1.35 us (2%)
  local copies, waits for them, and re-layouts  1.15 us (2%)
    ppermute x16, starting transfers between devices, run(): got.append(lax.ppermute(packs[2 * axis + odd], ('gx', 'gy'), pairs))  20.8 us
    ppermute x16, waiting for transfers between devices, run(): got.append(lax.ppermute(packs[2 * axis + odd], ('gx', 'gy'), pairs))  14.1 us
    all_to_all x1, starting transfers between devices, body(): sums = lax.all_to_all(sums, ('gx', 'gy'), 0, 0, tiled=True)  10.2 us
    all_to_all x1, waiting for transfers between devices, body(): sums = lax.all_to_all(sums, ('gx', 'gy'), 0, 0, tiled=True)  6.56 us
    pallas_call x4, Pallas kernels, call(): pl.pallas_call(kernel, name='level', in_specs=[SSPEC] + [VSPEC] * 4 + [pl...  4.68 us
    pallas_call x1, Pallas kernels, call(): pl.pallas_call(kernel, name='first', in_specs=[SSPEC, pl.BlockSpec(memory...  3.71 us
    ppermute x1, starting transfers between devices, body(): color_y = lax.ppermute(coloring, 'gy', [(j, j ^ 1) for j in range(plan.ny)])  2.64 us
  transfers between devices with their start and end apart: 19, of which 7 were waited for; matrix products, arithmetic and copies ran while one was open for 1% of the time, Pallas kernels for 0%

profile of v1, /device:TPU:0, one launch (start us, length us, event | category | flops | bytes accessed | tf_op | source)
XLA Modules:
  0.0 68.5 jit_solution(3742949805140000838)
XLA Ops:
  1.2 2.6 %collective-permute-start.17 = (s32[1,1]{1,0:T(1,128)}, s32[1,1]{1,0:T(1,128)}, u32[]{:S(2)}, u32[]{:S(2)}) collective-permute-start(s32[1,1]{1,0:T(1,128)} %param.19), channel_id=1, source_target_pairs={{0,1},{1,0},{2,3},{3,2},{4,5},{5,4},{6,7},{7,6},{8,9},{9,8},{10,11... | collective-permute-start | bytes 20 | tf_op jit(solution)/shard_map/ppermute | solution.py:390
  4.5 1.1 %collective-permute-done.17.color_y = s32[1,1]{1,0:T(1,128)} collective-permute-done((s32[1,1]{1,0:T(1,128)}, s32[1,1]{1,0:T(1,128)}, u32[]{:S(2)}, u32[]{:S(2)}) %collective-permute-start.17) | collective-permute-done | bytes 36 | tf_op jit(solution)/shard_map/ppermute | solution.py:390
  5.6 3.7 %first.1 = (s32[1]{0:T(128)S(4)}, s32[2]{0:T(128)S(4)}, bf16[75,125,128]{2,1,0:T(8,128)(2,1)S(1)}, f32[536,128]{1,0:T(8,128)S(1)}, bf16[768,128]{1,0:T(8,128)(2,...) custom-call(s32[1,1]{1,0:T(1,128)S(6)} %copy.48.color, ...), custom_call_target="tpu_custom_call" | custom-call | tf_op jit(solution)/shard_map/first/pallas_call | solution.py:229
  9.3 40.5 %while.20 = (s32[]{:T(128)S(4)}, f32[536,128]{1,0:T(8,128)S(1)}, f32[64,128]{1,0:T(8,128)S(1)}, f32[64,128]{1,0:T(8,128)S(1)}, f32[64,128]{1,0:T(8,128)S(1)}, /*...) while((s32[]{:T(128)S(4)}, f32[536,128]{1,0:T(8,128)S(1)}, ...), condition=%wide.region_7.0_spmd, body=%wide.region_0.0_spmd.sunk | while | flops 5 | bytes 524733 | solution.py:408
  9.4 7.9 %conditional.2 = (f32[536,128]{1,0:T(8,128)S(1)}) conditional(s32[]{:T(128)} %clamp.7, (f32[64,128]{1,0:T(8,128)S(1)}, f32[64,128]{1,0:T(8,128)S(1)}, f32[536,128]{1,0:T(8,128)S(1)}) %tuple.51, (f32[64,128]{1,0:T(8,128)S(1)}, f32[64,128]{1,0:T(8,128)S(1)}, f32[536,128]{1,0:T(8,128)S(1)}) %tuple.52, ...), branch_computations={%region_1.0_spmd, %region_2.0_spmd, %region_3.0_spmd, %region_4.0_... | conditional | bytes 524456 | solution.py:404
  9.4 1.3 %collective-permute-start.12 = (f32[64,128]{1,0:T(8,128)S(1)}, f32[64,128]{1,0:T(8,128)S(1)}, u32[]{:S(2)}, u32[]{:S(2)}) collective-permute-start(f32[64,128]{1,0:T(8,128)S(1)} %get-tuple-element.199), channel_id=1, source_target_pairs={{4,0},{1,5},{6,2},{3,7},{12,8},{9,13},{14,10},{11,15},{20,16},{17,... | collective-permute-start | bytes 98312 | tf_op jit(solution)/shard_map/while/body/cond/branch_5_fun/ppermute | solution.py:379
  10.7 0.7 collective-permute-start.13
  11.4 1.3 %collective-permute-start.14 = (f32[64,128]{1,0:T(8,128)S(1)}, f32[64,128]{1,0:T(8,128)S(1)}, u32[]{:S(2)}, u32[]{:S(2)}) collective-permute-start(f32[64,128]{1,0:T(8,128)S(1)} %get-tuple-element.201), channel_id=1, source_target_pairs={{1,0},{3,2},{4,5},{6,7},{9,8},{11,10},{12,13},{14,15},{17,16},{19,... | collective-permute-start | bytes 98312 | tf_op jit(solution)/shard_map/while/body/cond/branch_5_fun/ppermute | solution.py:379
  12.7 0.7 collective-permute-start.15
  13.4 3.8 %collective-permute-done.14.refs_3_ = f32[64,128]{1,0:T(8,128)S(1)} collective-permute-done((f32[64,128]{1,0:T(8,128)S(1)}, f32[64,128]{1,0:T(8,128)S(1)}, u32[]{:S(2)}, u32[]{:S(2)}) %collective-permute-start.14) | collective-permute-done | bytes 32800 | tf_op jit(solution)/shard_map/while/body/cond/branch_5_fun/ppermute | solution.py:379
  17.3 2.1 %level.4 = (f32[536,128]{1,0:T(8,128)S(1)}, f32[64,128]{1,0:T(8,128)S(1)}, f32[64,128]{1,0:T(8,128)S(1)}, f32[64,128]{1,0:T(8,128)S(1)}, f32[64,128]{1,0:T(8,128)S(1)}) custom-call(s32[2]{0:T(128)S(4)} %get-tuple-element.386.control, f32[536,128]{1,0:T(8,128)S(1)} %get-tuple-element.397.old_state, ...), custom_call_target="tpu_custom_call", output_to_operand_aliasing={{0}: (1, {})} | custom-call | tf_op jit(solution)/shard_map/while/body/level/pallas_call | solution.py:306
  19.5 7.5 %conditional.2 = (f32[536,128]{1,0:T(8,128)S(1)}) conditional(s32[]{:T(128)} %clamp.7, (f32[64,128]{1,0:T(8,128)S(1)}, f32[64,128]{1,0:T(8,128)S(1)}, f32[536,128]{1,0:T(8,128)S(1)}) %tuple.51, (f32[64,128]{1,0:T(8,128)S(1)}, f32[64,128]{1,0:T(8,128)S(1)}, f32[536,128]{1,0:T(8,128)S(1)}) %tuple.52, ...), branch_computations={%region_1.0_spmd, %region_2.0_spmd, %region_3.0_spmd, %region_4.0_... | conditional | bytes 524456 | solution.py:404
  19.5 1.3 %collective-permute-start.8 = (f32[64,128]{1,0:T(8,128)S(1)}, f32[64,128]{1,0:T(8,128)S(1)}, u32[]{:S(2)}, u32[]{:S(2)}) collective-permute-start(f32[64,128]{1,0:T(8,128)S(1)} %get-tuple-element.194), channel_id=1, source_target_pairs={{0,4},{5,1},{2,6},{7,3},{8,12},{13,9},{10,14},{15,11},{16,20},{21,... | collective-permute-start | bytes 98312 | tf_op jit(solution)/shard_map/while/body/cond/branch_4_fun/ppermute | solution.py:379
  20.8 0.7 collective-permute-start.9
  21.5 3.9 %collective-permute-start.10 = (f32[64,128]{1,0:T(8,128)S(1)}, f32[64,128]{1,0:T(8,128)S(1)}, u32[]{:S(2)}, u32[]{:S(2)}) collective-permute-start(f32[64,128]{1,0:T(8,128)S(1)} %get-tuple-element.196), channel_id=1, source_target_pairs={{0,1},{2,3},{5,4},{7,6},{8,9},{10,11},{13,12},{15,14},{16,17},{18,... | collective-permute-start | bytes 98312 | tf_op jit(solution)/shard_map/while/body/cond/branch_4_fun/ppermute | solution.py:379
  25.4 0.7 collective-permute-start.11
  26.1 0.9 %collective-permute-done.10.refs_3_ = f32[64,128]{1,0:T(8,128)S(1)} collective-permute-done((f32[64,128]{1,0:T(8,128)S(1)}, f32[64,128]{1,0:T(8,128)S(1)}, u32[]{:S(2)}, u32[]{:S(2)}) %collective-permute-start.10) | collective-permute-done | bytes 32800 | tf_op jit(solution)/shard_map/while/body/cond/branch_4_fun/ppermute | solution.py:379
  27.3 12.6 %conditional.2 = (f32[536,128]{1,0:T(8,128)S(1)}) conditional(s32[]{:T(128)} %clamp.7, (f32[64,128]{1,0:T(8,128)S(1)}, f32[64,128]{1,0:T(8,128)S(1)}, f32[536,128]{1,0:T(8,128)S(1)}) %tuple.51, (f32[64,128]{1,0:T(8,128)S(1)}, f32[64,128]{1,0:T(8,128)S(1)}, f32[536,128]{1,0:T(8,128)S(1)}) %tuple.52, ...), branch_computations={%region_1.0_spmd, %region_2.0_spmd, %region_3.0_spmd, %region_4.0_... | conditional | bytes 524456 | solution.py:404
  27.3 1.3 %collective-permute-start.12 = (f32[64,128]{1,0:T(8,128)S(1)}, f32[64,128]{1,0:T(8,128)S(1)}, u32[]{:S(2)}, u32[]{:S(2)}) collective-permute-start(f32[64,128]{1,0:T(8,128)S(1)} %get-tuple-element.199), channel_id=1, source_target_pairs={{4,0},{1,5},{6,2},{3,7},{12,8},{9,13},{14,10},{11,15},{20,16},{17,... | collective-permute-start | bytes 98312 | tf_op jit(solution)/shard_map/while/body/cond/branch_5_fun/ppermute | solution.py:379
  28.6 0.7 collective-permute-start.13
  29.3 1.3 %collective-permute-start.14 = (f32[64,128]{1,0:T(8,128)S(1)}, f32[64,128]{1,0:T(8,128)S(1)}, u32[]{:S(2)}, u32[]{:S(2)}) collective-permute-start(f32[64,128]{1,0:T(8,128)S(1)} %get-tuple-element.201), channel_id=1, source_target_pairs={{1,0},{3,2},{4,5},{6,7},{9,8},{11,10},{12,13},{14,15},{17,16},{19,... | collective-permute-start | bytes 98312 | tf_op jit(solution)/shard_map/while/body/cond/branch_5_fun/ppermute | solution.py:379
  30.6 0.7 collective-permute-start.15
  31.2 3.1 %collective-permute-done.12.refs_1_ = f32[64,128]{1,0:T(8,128)S(1)} collective-permute-done((f32[64,128]{1,0:T(8,128)S(1)}, f32[64,128]{1,0:T(8,128)S(1)}, u32[]{:S(2)}, u32[]{:S(2)}) %collective-permute-start.12) | collective-permute-done | bytes 32800 | tf_op jit(solution)/shard_map/while/body/cond/branch_5_fun/ppermute | solution.py:379
  34.3 5.5 %collective-permute-done.14.refs_3_ = f32[64,128]{1,0:T(8,128)S(1)} collective-permute-done((f32[64,128]{1,0:T(8,128)S(1)}, f32[64,128]{1,0:T(8,128)S(1)}, u32[]{:S(2)}, u32[]{:S(2)}) %collective-permute-start.14) | collective-permute-done | bytes 32800 | tf_op jit(solution)/shard_map/while/body/cond/branch_5_fun/ppermute | solution.py:379
  39.9 2.1 %level.4 = (f32[536,128]{1,0:T(8,128)S(1)}, f32[64,128]{1,0:T(8,128)S(1)}, f32[64,128]{1,0:T(8,128)S(1)}, f32[64,128]{1,0:T(8,128)S(1)}, f32[64,128]{1,0:T(8,128)S(1)}) custom-call(s32[2]{0:T(128)S(4)} %get-tuple-element.386.control, f32[536,128]{1,0:T(8,128)S(1)} %get-tuple-element.397.old_state, ...), custom_call_target="tpu_custom_call", output_to_operand_aliasing={{0}: (1, {})} | custom-call | tf_op jit(solution)/shard_map/while/body/level/pallas_call | solution.py:306
  42.0 7.5 %conditional.2 = (f32[536,128]{1,0:T(8,128)S(1)}) conditional(s32[]{:T(128)} %clamp.7, (f32[64,128]{1,0:T(8,128)S(1)}, f32[64,128]{1,0:T(8,128)S(1)}, f32[536,128]{1,0:T(8,128)S(1)}) %tuple.51, (f32[64,128]{1,0:T(8,128)S(1)}, f32[64,128]{1,0:T(8,128)S(1)}, f32[536,128]{1,0:T(8,128)S(1)}) %tuple.52, ...), branch_computations={%region_1.0_spmd, %region_2.0_spmd, %region_3.0_spmd, %region_4.0_... | conditional | bytes 524456 | solution.py:404
  42.1 1.3 %collective-permute-start.8 = (f32[64,128]{1,0:T(8,128)S(1)}, f32[64,128]{1,0:T(8,128)S(1)}, u32[]{:S(2)}, u32[]{:S(2)}) collective-permute-start(f32[64,128]{1,0:T(8,128)S(1)} %get-tuple-element.194), channel_id=1, source_target_pairs={{0,4},{5,1},{2,6},{7,3},{8,12},{13,9},{10,14},{15,11},{16,20},{21,... | collective-permute-start | bytes 98312 | tf_op jit(solution)/shard_map/while/body/cond/branch_4_fun/ppermute | solution.py:379
  44.1 3.9 %collective-permute-start.10 = (f32[64,128]{1,0:T(8,128)S(1)}, f32[64,128]{1,0:T(8,128)S(1)}, u32[]{:S(2)}, u32[]{:S(2)}) collective-permute-start(f32[64,128]{1,0:T(8,128)S(1)} %get-tuple-element.196), channel_id=1, source_target_pairs={{0,1},{2,3},{5,4},{7,6},{8,9},{10,11},{13,12},{15,14},{16,17},{18,... | collective-permute-start | bytes 98312 | tf_op jit(solution)/shard_map/while/body/cond/branch_4_fun/ppermute | solution.py:379
  48.6 0.9 %collective-permute-done.10.refs_3_ = f32[64,128]{1,0:T(8,128)S(1)} collective-permute-done((f32[64,128]{1,0:T(8,128)S(1)}, f32[64,128]{1,0:T(8,128)S(1)}, u32[]{:S(2)}, u32[]{:S(2)}) %collective-permute-start.10) | collective-permute-done | bytes 32800 | tf_op jit(solution)/shard_map/while/body/cond/branch_4_fun/ppermute | solution.py:379
  49.8 0.7 %last.1 = (f32[125,1,128]{2,1,0:T(1,128)S(1)}, f32[32,128]{1,0:T(8,128)}) custom-call(f32[536,128]{1,0:T(8,128)S(1)} %get-tuple-element.245.state), custom_call_target="tpu_custom_call" | custom-call | tf_op jit(solution)/shard_map/last/pallas_call | solution.py:336
  50.5 10.2 %all-to-all-start = ((f32[32,1,128]{2,1,0:T(1,128)}), f32[32,1,128]{2,1,0:T(1,128)S(1)}, u32[]{:S(2)}, u32[]{:S(2)}) async-start(f32[32,1,128]{2,1,0:T(1,128)} %bitcast.9), calls=%async_computation | async-start | bytes 32768 | tf_op jit(solution)/shard_map/all_to_all | solution.py:410
  61.4 6.6 %all-to-all-done = f32[32,1,128]{2,1,0:T(1,128)S(1)} async-done(((f32[32,1,128]{2,1,0:T(1,128)}), f32[32,1,128]{2,1,0:T(1,128)S(1)}, u32[]{:S(2)}, u32[]{:S(2)}) %all-to-all-start) | async-done | bytes 16416 | tf_op jit(solution)/shard_map/all_to_all | solution.py:410
  (24 shorter events, 3.8 us)
Async XLA Ops:
  0.6 3.9 %collective-permute-start.16 = (s32[1,1]{1,0:T(1,128)}, s32[1,1]{1,0:T(1,128)}, u32[]{:S(2)}, u32[]{:S(2)}) collective-permute-start(s32[1,1]{1,0:T(1,128)} %param.19), channel_id=1, source_target_pairs={{0,4},{4,0},{8,12},{12,8},{16,20},{20,16},{24,28},{28,24},{1,5},{5... | collective-permute-start | bytes 20 | tf_op jit(solution)/shard_map/ppermute | solution.py:389
  1.2 4.4 %collective-permute-start.17 = (s32[1,1]{1,0:T(1,128)}, s32[1,1]{1,0:T(1,128)}, u32[]{:S(2)}, u32[]{:S(2)}) collective-permute-start(s32[1,1]{1,0:T(1,128)} %param.19), channel_id=1, source_target_pairs={{0,1},{1,0},{2,3},{3,2},{4,5},{5,4},{6,7},{7,6},{8,9},{9,8},{10,11... | collective-permute-start | bytes 20 | tf_op jit(solution)/shard_map/ppermute | solution.py:390
  9.4 3.9 %collective-permute-start.12 = (f32[64,128]{1,0:T(8,128)S(1)}, f32[64,128]{1,0:T(8,128)S(1)}, u32[]{:S(2)}, u32[]{:S(2)}) collective-permute-start(f32[64,128]{1,0:T(8,128)S(1)} %get-tuple-element.199), channel_id=1, source_target_pairs={{4,0},{1,5},{6,2},{3,7},{12,8},{9,13},{14,10},{11,15},{20,16},{17,... | collective-permute-start | bytes 98312 | tf_op jit(solution)/shard_map/while/body/cond/branch_5_fun/ppermute | solution.py:379
  10.7 2.7 %collective-permute-start.13 = (f32[64,128]{1,0:T(8,128)S(1)}, f32[64,128]{1,0:T(8,128)S(1)}, u32[]{:S(2)}, u32[]{:S(2)}) collective-permute-start(f32[64,128]{1,0:T(8,128)S(1)} %get-tuple-element.200), channel_id=1, source_target_pairs={{4,8},{9,5},{6,10},{11,7},{12,16},{17,13},{14,18},{19,15},{20,24},... | collective-permute-start | bytes 98312 | tf_op jit(solution)/shard_map/while/body/cond/branch_5_fun/ppermute | solution.py:379
  11.4 5.8 %collective-permute-start.14 = (f32[64,128]{1,0:T(8,128)S(1)}, f32[64,128]{1,0:T(8,128)S(1)}, u32[]{:S(2)}, u32[]{:S(2)}) collective-permute-start(f32[64,128]{1,0:T(8,128)S(1)} %get-tuple-element.201), channel_id=1, source_target_pairs={{1,0},{3,2},{4,5},{6,7},{9,8},{11,10},{12,13},{14,15},{17,16},{19,... | collective-permute-start | bytes 98312 | tf_op jit(solution)/shard_map/while/body/cond/branch_5_fun/ppermute | solution.py:379
  12.7 4.5 %collective-permute-start.15 = (f32[64,128]{1,0:T(8,128)S(1)}, f32[64,128]{1,0:T(8,128)S(1)}, u32[]{:S(2)}, u32[]{:S(2)}) collective-permute-start(f32[64,128]{1,0:T(8,128)S(1)} %get-tuple-element.202), channel_id=1, source_target_pairs={{1,2},{2,1},{5,6},{6,5},{9,10},{10,9},{13,14},{14,13},{17,18},{18,... | collective-permute-start | bytes 98312 | tf_op jit(solution)/shard_map/while/body/cond/branch_5_fun/ppermute | solution.py:379
  19.5 6.5 %collective-permute-start.8 = (f32[64,128]{1,0:T(8,128)S(1)}, f32[64,128]{1,0:T(8,128)S(1)}, u32[]{:S(2)}, u32[]{:S(2)}) collective-permute-start(f32[64,128]{1,0:T(8,128)S(1)} %get-tuple-element.194), channel_id=1, source_target_pairs={{0,4},{5,1},{2,6},{7,3},{8,12},{13,9},{10,14},{15,11},{16,20},{21,... | collective-permute-start | bytes 98312 | tf_op jit(solution)/shard_map/while/body/cond/branch_4_fun/ppermute | solution.py:379
  20.8 5.2 %collective-permute-start.9 = (f32[64,128]{1,0:T(8,128)S(1)}, f32[64,128]{1,0:T(8,128)S(1)}, u32[]{:S(2)}, u32[]{:S(2)}) collective-permute-start(f32[64,128]{1,0:T(8,128)S(1)} %get-tuple-element.195), channel_id=1, source_target_pairs={{8,4},{5,9},{10,6},{7,11},{16,12},{13,17},{18,14},{15,19},{24,20},... | collective-permute-start | bytes 98312 | tf_op jit(solution)/shard_map/while/body/cond/branch_4_fun/ppermute | solution.py:379
  21.5 5.5 %collective-permute-start.10 = (f32[64,128]{1,0:T(8,128)S(1)}, f32[64,128]{1,0:T(8,128)S(1)}, u32[]{:S(2)}, u32[]{:S(2)}) collective-permute-start(f32[64,128]{1,0:T(8,128)S(1)} %get-tuple-element.196), channel_id=1, source_target_pairs={{0,1},{2,3},{5,4},{7,6},{8,9},{10,11},{13,12},{15,14},{16,17},{18,... | collective-permute-start | bytes 98312 | tf_op jit(solution)/shard_map/while/body/cond/branch_4_fun/ppermute | solution.py:379
  25.4 1.6 %collective-permute-start.11 = (f32[64,128]{1,0:T(8,128)S(1)}, f32[64,128]{1,0:T(8,128)S(1)}, u32[]{:S(2)}, u32[]{:S(2)}) collective-permute-start(f32[64,128]{1,0:T(8,128)S(1)} %get-tuple-element.197), channel_id=1, source_target_pairs={{1,2},{2,1},{5,6},{6,5},{9,10},{10,9},{13,14},{14,13},{17,18},{18,... | collective-permute-start | bytes 98312 | tf_op jit(solution)/shard_map/while/body/cond/branch_4_fun/ppermute | solution.py:379
  27.3 7.0 %collective-permute-start.12 = (f32[64,128]{1,0:T(8,128)S(1)}, f32[64,128]{1,0:T(8,128)S(1)}, u32[]{:S(2)}, u32[]{:S(2)}) collective-permute-start(f32[64,128]{1,0:T(8,128)S(1)} %get-tuple-element.199), channel_id=1, source_target_pairs={{4,0},{1,5},{6,2},{3,7},{12,8},{9,13},{14,10},{11,15},{20,16},{17,... | collective-permute-start | bytes 98312 | tf_op jit(solution)/shard_map/while/body/cond/branch_5_fun/ppermute | solution.py:379
  28.6 5.7 %collective-permute-start.13 = (f32[64,128]{1,0:T(8,128)S(1)}, f32[64,128]{1,0:T(8,128)S(1)}, u32[]{:S(2)}, u32[]{:S(2)}) collective-permute-start(f32[64,128]{1,0:T(8,128)S(1)} %get-tuple-element.200), channel_id=1, source_target_pairs={{4,8},{9,5},{6,10},{11,7},{12,16},{17,13},{14,18},{19,15},{20,24},... | collective-permute-start | bytes 98312 | tf_op jit(solution)/shard_map/while/body/cond/branch_5_fun/ppermute | solution.py:379
  29.3 10.5 %collective-permute-start.14 = (f32[64,128]{1,0:T(8,128)S(1)}, f32[64,128]{1,0:T(8,128)S(1)}, u32[]{:S(2)}, u32[]{:S(2)}) collective-permute-start(f32[64,128]{1,0:T(8,128)S(1)} %get-tuple-element.201), channel_id=1, source_target_pairs={{1,0},{3,2},{4,5},{6,7},{9,8},{11,10},{12,13},{14,15},{17,16},{19,... | collective-permute-start | bytes 98312 | tf_op jit(solution)/shard_map/while/body/cond/branch_5_fun/ppermute | solution.py:379
  30.6 9.2 %collective-permute-start.15 = (f32[64,128]{1,0:T(8,128)S(1)}, f32[64,128]{1,0:T(8,128)S(1)}, u32[]{:S(2)}, u32[]{:S(2)}) collective-permute-start(f32[64,128]{1,0:T(8,128)S(1)} %get-tuple-element.202), channel_id=1, source_target_pairs={{1,2},{2,1},{5,6},{6,5},{9,10},{10,9},{13,14},{14,13},{17,18},{18,... | collective-permute-start | bytes 98312 | tf_op jit(solution)/shard_map/while/body/cond/branch_5_fun/ppermute | solution.py:379
  42.1 6.5 %collective-permute-start.8 = (f32[64,128]{1,0:T(8,128)S(1)}, f32[64,128]{1,0:T(8,128)S(1)}, u32[]{:S(2)}, u32[]{:S(2)}) collective-permute-start(f32[64,128]{1,0:T(8,128)S(1)} %get-tuple-element.194), channel_id=1, source_target_pairs={{0,4},{5,1},{2,6},{7,3},{8,12},{13,9},{10,14},{15,11},{16,20},{21,... | collective-permute-start | bytes 98312 | tf_op jit(solution)/shard_map/while/body/cond/branch_4_fun/ppermute | solution.py:379
  43.4 5.2 %collective-permute-start.9 = (f32[64,128]{1,0:T(8,128)S(1)}, f32[64,128]{1,0:T(8,128)S(1)}, u32[]{:S(2)}, u32[]{:S(2)}) collective-permute-start(f32[64,128]{1,0:T(8,128)S(1)} %get-tuple-element.195), channel_id=1, source_target_pairs={{8,4},{5,9},{10,6},{7,11},{16,12},{13,17},{18,14},{15,19},{24,20},... | collective-permute-start | bytes 98312 | tf_op jit(solution)/shard_map/while/body/cond/branch_4_fun/ppermute | solution.py:379
  44.1 5.5 %collective-permute-start.10 = (f32[64,128]{1,0:T(8,128)S(1)}, f32[64,128]{1,0:T(8,128)S(1)}, u32[]{:S(2)}, u32[]{:S(2)}) collective-permute-start(f32[64,128]{1,0:T(8,128)S(1)} %get-tuple-element.196), channel_id=1, source_target_pairs={{0,1},{2,3},{5,4},{7,6},{8,9},{10,11},{13,12},{15,14},{16,17},{18,... | collective-permute-start | bytes 98312 | tf_op jit(solution)/shard_map/while/body/cond/branch_4_fun/ppermute | solution.py:379
  47.9 1.6 %collective-permute-start.11 = (f32[64,128]{1,0:T(8,128)S(1)}, f32[64,128]{1,0:T(8,128)S(1)}, u32[]{:S(2)}, u32[]{:S(2)}) collective-permute-start(f32[64,128]{1,0:T(8,128)S(1)} %get-tuple-element.197), channel_id=1, source_target_pairs={{1,2},{2,1},{5,6},{6,5},{9,10},{10,9},{13,14},{14,13},{17,18},{18,... | collective-permute-start | bytes 98312 | tf_op jit(solution)/shard_map/while/body/cond/branch_4_fun/ppermute | solution.py:379
  50.5 17.4 %all-to-all-start = ((f32[32,1,128]{2,1,0:T(1,128)}), f32[32,1,128]{2,1,0:T(1,128)S(1)}, u32[]{:S(2)}, u32[]{:S(2)}) async-start(f32[32,1,128]{2,1,0:T(1,128)} %bitcast.9), calls=%async_computation | async-start | bytes 32768 | tf_op jit(solution)/shard_map/all_to_all | solution.py:410
